TPU v7x, 32 devices: a whole 2x2x4 slice. The times are simulated.
32 devices in a mesh: shot: 4 (over y, core), space: 8 (over z, x).
Axes of the slice: x: 2, y: 2, z: 4, core: 2. Of those that a mesh axis runs over, the one named last changes fastest.
Arguments:
- adjoint_now: float32 [4, 128, 64, 512], P('shot', 'space'), may hold values from -6 to 6
- adjoint_later: float32 [4, 128, 64, 512], P('shot', 'space'), may hold values from -6 to 6
- courant: float32 [128, 64, 512], P('space'), may hold values from 0.05 to 0.2
- checkpoint_codes: int32 [4, 6, 128, 64, 128], P('shot', None, 'space'), may hold values from -2147483648 to 2147483646
- scale_index: int32 [4, 6, 128, 256], P('shot', None, 'space'), may hold values from 0 to 63
- scale_table: float32 [64], replicated, may hold values from 0.001 to 0.01
- receiver_cell: int32 [4, 2048], P('shot', 'space'), may hold values from 0 to 4194303, as said below
- observed: float32 [4, 4, 2048], P('shot', None, 'space'), may hold values from -12 to 12
- source_cell: int32 [4, 3], P('shot'), may hold values from 0 to 511, as said below
Outputs:
- gradient: float32 [128, 64, 512], P('space', 'shot')
- adjoint_first: float32 [4, 128, 64, 512], P('shot', 'space')
- adjoint_second: float32 [4, 128, 64, 512], P('shot', 'space')
- misfit: float32 [], replicated
Inputs may be any that keep to these rules, and one draw needn't show every extreme that they name: `receiver_cell`: for every r, entries r * 256 to (r + 1) * 256 - 1 of each shot's row are flat indices (z * 64 + y) * 512 + x of cells with r * 16 <= z < (r + 1) * 16. `source_cell`: column 0 is a z index below 128, column 1 a y index below 64, column 2 an x index below 512.
All inputs are finite; a program needn't handle non-finite values.
Results may differ from a plain program's by a relative error of at most 0.0001.
Values sent between devices are 32-bit elements; how exact they have to be, the bound alone decides.
A program may use at most 128 MiB of HBM per device.

v0:
```python
import functools

import jax
import jax.numpy as jnp
from jax import lax
from jax.experimental import pallas as pl
from jax.experimental.pallas import tpu as pltpu
from jax.sharding import PartitionSpec as P

ITERS = 4
QBLOCK = 128
MUTE = 8
W = 4
NC = 2
F32 = jnp.float32
BF16 = jnp.bfloat16
MESH = pl.DeviceIdType.MESH

COEFFS = (-205.0 / 72.0, 8.0 / 5.0, -1.0 / 5.0, 8.0 / 315.0, -1.0 / 560.0)


def split(value):
    high = value.astype(BF16)
    return high, (value - high.astype(F32)).astype(BF16)


def dot(a, b):
    return jnp.dot(a, b, preferred_element_type=F32)


def band(rows, cols, first):
    i = first + lax.broadcasted_iota(jnp.int32, (rows, cols), 0)
    j = lax.broadcasted_iota(jnp.int32, (rows, cols), 1)
    d = jnp.abs(i - j)
    value = jnp.zeros((rows, cols), F32)
    for k in range(1, 5):
        value = jnp.where(d == k, COEFFS[k], value)
    return split(value)


def kernel(
    nshot,
    nspace,
    cells_s,
    source_s,
    table,
    observed,
    now_h,
    later_h,
    cour_h,
    words_h,
    index,
    cells_row,
    grad,
    first_h,
    second_h,
    misfit,
    E,
    D,
    cour,
    words,
    SC,
    TS,
    PC,
    OB,
    IM,
    RA,
    S,
    RB,
    PR,
    QH,
    QL,
    CH,
    CL,
    GW,
    GS,
    MB,
    SB,
    MT,
    ST,
    halo_send,
    halo_recv,
    a_send,
    a_recv,
    b_send,
    b_recv,
    m_send,
    m_recv,
    s_send,
    s_recv,
    local_sem,
):
    depth, rows, cols = cour.shape
    nrec = cells_row.shape[1]
    blocks = cols // QBLOCK
    ych = rows // NC
    shot = lax.axis_index("shot")
    space = lax.axis_index("space")
    has_low = space > 0
    has_high = space < nspace - 1

    barrier = pltpu.get_barrier_semaphore()
    for d in range(1, nshot):
        pl.semaphore_signal(
            barrier, inc=1, device_id={"shot": lax.rem(shot + d, nshot)}, device_id_type=MESH
        )

    @pl.loop(1, nspace)
    def _(d):
        pl.semaphore_signal(
            barrier, inc=1, device_id={"space": lax.rem(space + d, nspace)}, device_id_type=MESH
        )

    in_now = pltpu.make_async_copy(now_h, E.at[1, pl.ds(W, depth)], local_sem.at[0])
    in_later = pltpu.make_async_copy(later_h, E.at[0, pl.ds(W, depth)], local_sem.at[1])
    in_cour = pltpu.make_async_copy(cour_h, cour, local_sem.at[2])
    in_words = pltpu.make_async_copy(words_h, words, local_sem.at[3])
    in_words.start()
    in_now.start()
    in_cour.start()
    in_later.start()

    pl.semaphore_wait(barrier, nshot + nspace - 2)

    def halo(t, c, up):
        ys = pl.ds(c * ych, ych)
        src_z = W + depth - W if up else W
        dst_z = 0 if up else W + depth
        return pltpu.make_async_remote_copy(
            src_ref=E.at[t + 1, pl.ds(src_z, W), ys, :],
            dst_ref=E.at[t + 1, pl.ds(dst_z, W), ys, :],
            send_sem=halo_send.at[int(up), t, c],
            recv_sem=halo_recv.at[int(up), t, c],
            device_id={"space": space + (1 if up else -1)},
            device_id_type=MESH,
        )

    def halo_first(c, up):
        ys = pl.ds(c * ych, ych)
        src_z = depth - W if up else 0
        dst_z = 0 if up else W + depth
        return pltpu.make_async_remote_copy(
            src_ref=now_h.at[pl.ds(src_z, W), ys, :],
            dst_ref=E.at[1, pl.ds(dst_z, W), ys, :],
            send_sem=halo_send.at[int(up), 0, c],
            recv_sem=halo_recv.at[int(up), 0, c],
            device_id={"space": space + (1 if up else -1)},
            device_id_type=MESH,
        )

    for c in range(NC):

        @pl.when(has_high)
        def _():
            halo_first(c, True).start()

        @pl.when(has_low)
        def _():
            halo_first(c, False).start()

    @pl.loop(0, cols // 64)
    def _(i):
        start = pl.multiple_of(i * 64, 64)
        high, low = band(64, cols, start)
        CH[pl.ds(start, 64), :] = high
        CL[pl.ds(start, 64), :] = low

    yh, yl = band(rows, rows, 0)

    entry = index[...]
    scale = jnp.zeros(entry.shape, F32)
    for e in range(table.shape[0]):
        scale = jnp.where(entry == e, table[e], scale)
    levels = entry.shape[0]
    SC[0:levels] = scale
    SC[levels:] = jnp.zeros((SC.shape[0] - levels,) + entry.shape[1:], F32)

    slab = depth * rows * cols
    in_words.wait()

    @pl.loop(0, nrec, unroll=4)
    def _(r):
        cell = lax.rem(cells_s[r], slab)
        row = cell // cols
        z = row // rows
        y = lax.rem(row, rows)
        for k in range(1, ITERS + 1):
            GW[k - 1, pl.ds(r, 1), :] = words[k, z, pl.ds(y, 1), :]
            GS[k - 1, pl.ds(r, 1), :] = SC[k, pl.ds(z, 1), :]
            OB[k - 1, pl.ds(r, 1), :] = jnp.full((1, 128), observed[k - 1, r], F32)
        PC[pl.ds(r, 1), :] = jnp.full((1, 128), cell - z * (rows * cols), jnp.int32)

    place = PC[:, 0:1]
    xcol = lax.rem(place, cols)
    mcol = xcol // QBLOCK
    jcol = lax.rem(xcol, QBLOCK)
    scol = place // cols * blocks + mcol
    lane = lax.broadcasted_iota(jnp.int32, (nrec, QBLOCK), 1)
    sl = lax.broadcasted_iota(jnp.int32, (nrec, rows * blocks), 1)
    xl = lax.broadcasted_iota(jnp.int32, (nrec, cols), 1)
    squares = jnp.zeros((1, 1), F32)
    for k in range(1, ITERS + 1):
        code = jnp.bitwise_and(jnp.right_shift(GW[k - 1], 8 * mcol), 255) - 128
        code = jnp.sum(jnp.where(lane == jcol, code.astype(F32), 0.0), axis=1, keepdims=True)
        scale = jnp.sum(jnp.where(sl == scol, GS[k - 1], 0.0), axis=1, keepdims=True)
        residual = code * scale - OB[k - 1, :, 0:1]
        squares = squares + jnp.sum(residual * residual, axis=0, keepdims=True)
        high, low = split(jnp.where(xl == xcol, residual, 0.0))
        QH[ITERS - k] = high
        QL[ITERS - k] = low
    crow = lax.rem(cells_row[...], slab) // cols
    for z in range(depth):
        i = z * rows + lax.broadcasted_iota(jnp.int32, (rows, nrec), 0)
        PR[z] = jnp.where(i == crow, 1.0, 0.0).astype(BF16)

    tile = jnp.broadcast_to(squares, (8, 128))
    MT[...] = tile
    MB[pl.ds(shot, 1)] = tile.reshape(1, 8, 128)

    def misfit_copy(d):
        return pltpu.make_async_remote_copy(
            src_ref=MT,
            dst_ref=MB.at[shot],
            send_sem=m_send.at[d - 1],
            recv_sem=m_recv.at[d - 1],
            device_id={"shot": lax.rem(shot + d, nshot)},
            device_id_type=MESH,
        )

    def total_copy(d):
        return pltpu.make_async_remote_copy(
            src_ref=ST,
            dst_ref=SB.at[space],
            send_sem=s_send.at[d - 1],
            recv_sem=s_recv.at[d - 1],
            device_id={"space": lax.rem(space + d, nspace)},
            device_id_type=MESH,
        )

    for d in range(1, nshot):
        misfit_copy(d).start()

    in_now.wait()
    in_later.wait()
    in_cour.wait()

    def local(t):
        for g in (0, depth // W - 1) + tuple(range(1, depth // W - 1)):
            z0 = g * W
            u = E[t + 1, W + z0 : W + z0 + W].reshape(W * rows, cols)
            uh, ul = split(u)
            lap = dot(uh, CH[...]) + dot(ul, CH[...]) + dot(uh, CL[...])
            for j in range(W):
                z = z0 + j
                part = slice(j * rows, (j + 1) * rows)
                up = u[part]
                acc = lap[part] + (3.0 * COEFFS[0]) * up
                acc = acc + dot(yh, uh[part]) + dot(yh, ul[part]) + dot(yl, uh[part])
                for i in range(1, 5):
                    if z + i < depth:
                        acc = acc + COEFFS[i] * E[t + 1, W + z + i]
                    if z - i >= 0:
                        acc = acc + COEFFS[i] * E[t + 1, W + z - i]
                inject = dot(PR[z], QH[t]) + dot(PR[z], QL[t])
                E[t + 2, W + z] = 2.0 * up - E[t, W + z] + cour[z] * acc + inject

    local(0)

    def decode():
        i = lax.broadcasted_iota(jnp.int32, (rows, rows * blocks), 0)
        j = lax.broadcasted_iota(jnp.int32, (rows, rows * blocks), 1)
        flat = SC[...].reshape(128, rows * blocks)
        high = flat.astype(BF16)
        rest = flat - high.astype(F32)
        pieces = (high,) + split(rest)
        for m in range(blocks):
            pick = jnp.where(j == blocks * i + m, 1.0, 0.0).astype(BF16)
            moved = jnp.zeros((rows, 128), F32)
            for piece in pieces:
                moved = moved + lax.dot_general(
                    pick, piece, (((1,), (1,)), ((), ())), preferred_element_type=F32
                )
            TS[m] = moved

        @pl.loop(0, depth)
        def _(z):
            for m in range(blocks):
                xs = slice(m * QBLOCK, (m + 1) * QBLOCK)
                scale = pltpu.roll(TS[m], lax.rem(128 - z, 128), 1)
                f = []
                for k in range(ITERS + 2):
                    code = jnp.bitwise_and(jnp.right_shift(words[k, z], 8 * m), 255) - 128
                    f.append(code.astype(F32) * scale[:, k * depth : k * depth + 1])
                for t in range(ITERS):
                    k = ITERS - t
                    diff = f[k + 1] - 2.0 * f[k] + f[k - 1]
                    if t == 0:
                        IM[z, :, xs] = E[1, W + z, :, xs] * diff
                    else:
                        D[t - 1, z, :, xs] = diff

    for d in range(1, nshot):
        misfit_copy(d).wait()
    total = MB[0]
    for d in range(1, nshot):
        total = total + MB[d]
    ST[...] = total
    SB[pl.ds(space, 1)] = total.reshape(1, 8, 128)

    @pl.loop(1, nspace)
    def _(d):
        total_copy(d).start()

    def fix(t, c):
        ys = pl.ds(c * ych, ych)

        @pl.when(has_low)
        def _():
            halo(t, c, True).wait_recv()
            for j in range(W):
                acc = COEFFS[j + 1] * E[t + 1, W - 1, ys, :]
                for i in range(j + 2, 5):
                    acc = acc + COEFFS[i] * E[t + 1, W + j - i, ys, :]
                E[t + 2, W + j, ys, :] += cour[j, ys, :] * acc

        @pl.when(has_high)
        def _():
            halo(t, c, False).wait_recv()
            for j in range(W):
                z = depth - 1 - j
                acc = COEFFS[j + 1] * E[t + 1, W + depth, ys, :]
                for i in range(j + 2, 5):
                    acc = acc + COEFFS[i] * E[t + 1, W + z + i, ys, :]
                E[t + 2, W + z, ys, :] += cour[z, ys, :] * acc

    @pl.loop(0, ITERS - 1)
    def _(t):
        for c in range(NC):
            fix(t, c)

            @pl.when(has_high)
            def _():
                halo(t + 1, c, True).start()

            @pl.when(has_low)
            def _():
                halo(t + 1, c, False).start()

            if c == 0:

                @pl.when(t == 0)
                def _():
                    decode()

        local(t + 1)

        @pl.loop(0, depth)
        def _(z):
            IM[z] = IM[z] + E[t + 2, W + z] * D[t, z]

    out_second = pltpu.make_async_copy(E.at[ITERS, pl.ds(W, depth)], second_h, local_sem.at[4])
    out_second.start()
    inner = depth - 2 * W
    out_inner = pltpu.make_async_copy(
        E.at[ITERS + 1, pl.ds(2 * W, inner)], first_h.at[pl.ds(W, inner)], local_sem.at[5]
    )
    out_inner.start()

    first_z = space * depth

    @pl.loop(0, depth)
    def _(z):
        dz = first_z + z - source_s[0]
        dy = lax.broadcasted_iota(jnp.int32, (rows, cols), 0) - source_s[1]
        dx = lax.broadcasted_iota(jnp.int32, (rows, cols), 1) - source_s[2]
        dist = (dz * dz + dy * dy + dx * dx).astype(F32)
        IM[z] = IM[z] * (1.0 - jnp.exp(dist * (-1.0 / (2.0 * MUTE * MUTE))))

    core = lax.rem(shot, 2)
    pair = shot // 2
    pairs = nshot // 2
    yq = rows // nshot

    def quarter(index):
        return pl.ds(pl.multiple_of(index * yq, yq), yq)

    def copy_a(h):
        return pltpu.make_async_remote_copy(
            src_ref=IM.at[:, quarter(2 * h + 1 - core), :],
            dst_ref=RA.at[h],
            send_sem=a_send.at[h],
            recv_sem=a_recv.at[h],
            device_id={"shot": shot + 1 - 2 * core},
            device_id_type=MESH,
        )

    def copy_b(d):
        target = lax.rem(pair + d, pairs)
        return pltpu.make_async_remote_copy(
            src_ref=S.at[target],
            dst_ref=RB.at[d - 1],
            send_sem=b_send.at[d - 1],
            recv_sem=b_recv.at[d - 1],
            device_id={"shot": 2 * target + core},
            device_id_type=MESH,
        )

    for h in range(pairs):
        copy_a(h).start()
    for h in range(pairs):
        copy_a(h).wait()
        S[h] = IM[:, quarter(2 * h + core), :] + RA[h]
    for d in range(1, pairs):
        copy_b(d).start()

    for c in range(NC):
        fix(ITERS - 1, c)
    out_low = pltpu.make_async_copy(
        E.at[ITERS + 1, pl.ds(W, W)], first_h.at[pl.ds(0, W)], local_sem.at[6]
    )
    out_high = pltpu.make_async_copy(
        E.at[ITERS + 1, pl.ds(depth, W)], first_h.at[pl.ds(depth - W, W)], local_sem.at[7]
    )
    out_low.start()
    out_high.start()

    total = S[pair]
    for d in range(1, pairs):
        copy_b(d).wait()
        total = total + RB[d - 1]
    grad[...] = total

    @pl.loop(1, nspace)
    def _(d):
        total_copy(d).wait()

    whole = SB[0]
    for d in range(1, nspace):
        whole = whole + SB[d]
    misfit[...] = whole

    for c in range(NC):

        @pl.when(has_high)
        def _():
            halo_first(c, True).wait_send()

        @pl.when(has_low)
        def _():
            halo_first(c, False).wait_send()

        @pl.loop(1, ITERS)
        def _(t):
            @pl.when(has_high)
            def _():
                halo(t, c, True).wait_send()

            @pl.when(has_low)
            def _():
                halo(t, c, False).wait_send()

    out_second.wait()
    out_inner.wait()
    out_low.wait()
    out_high.wait()


def finish(factor, grad, first, second, total, grad_o, first_o, second_o, misfit, GB, FB, sem_in, sem_out):
    parts = FB.shape[0] // 2
    planes = FB.shape[1]
    moves = []
    for n, (source, target) in enumerate(((first, first_o), (second, second_o))):
        for p in range(parts):
            at = pl.ds(p * planes, planes)
            moves.append((source.at[at], FB.at[n * parts + p], target.at[at]))
    moves.append((grad, GB, grad_o))
    into = [
        pltpu.make_async_copy(source, held, sem_in.at[n])
        for n, (source, held, target) in enumerate(moves)
    ]
    out = [
        pltpu.make_async_copy(held, target, sem_out.at[n])
        for n, (source, held, target) in enumerate(moves)
    ]
    for copy in into:
        copy.start()
    misfit[...] = total[0:1, 0:1] * factor
    for n in range(len(moves)):
        into[n].wait()
        out[n].start()
    for copy in out:
        copy.wait()


def body(
    nshot,
    nspace,
    adjoint_now,
    adjoint_later,
    courant,
    checkpoint_codes,
    scale_index,
    scale_table,
    receiver_cell,
    observed,
    source_cell,
):
    depth, rows, cols = courant.shape
    levels = checkpoint_codes.shape[1]
    nrec = receiver_cell.shape[1]
    blocks = cols // QBLOCK
    pairs = nshot // 2
    yq = rows // nshot
    vmem = pl.BlockSpec(memory_space=pltpu.VMEM)
    smem = pl.BlockSpec(memory_space=pltpu.SMEM)
    anyspace = pl.BlockSpec(memory_space=pl.ANY)
    dma = pltpu.SemaphoreType.DMA
    field = jax.ShapeDtypeStruct((depth, rows, cols), F32)
    gradient, first, second, total = pl.pallas_call(
        functools.partial(kernel, nshot, nspace),
        out_shape=(
            jax.ShapeDtypeStruct((depth, yq, cols), F32),
            field,
            field,
            jax.ShapeDtypeStruct((8, 128), F32),
        ),
        in_specs=[smem] * 4 + [anyspace] * 4 + [vmem] * 2,
        out_specs=(vmem, anyspace, anyspace, vmem),
        scratch_shapes=[
            pltpu.VMEM((ITERS + 2, depth + 2 * W, rows, cols), F32),
            pltpu.VMEM((ITERS - 1, depth, rows, cols), F32),
            pltpu.VMEM((depth, rows, cols), F32),
            pltpu.VMEM((levels, depth, rows, QBLOCK), jnp.int32),
            pltpu.VMEM((128 // depth, depth, rows * blocks), F32),
            pltpu.VMEM((blocks, rows, 128), F32),
            pltpu.VMEM((nrec, 128), jnp.int32),
            pltpu.VMEM((ITERS, nrec, 128), F32),
            pltpu.VMEM((depth, rows, cols), F32),
            pltpu.VMEM((pairs, depth, yq, cols), F32),
            pltpu.VMEM((pairs, depth, yq, cols), F32),
            pltpu.VMEM((max(pairs - 1, 1), depth, yq, cols), F32),
            pltpu.VMEM((depth, rows, nrec), BF16),
            pltpu.VMEM((ITERS, nrec, cols), BF16),
            pltpu.VMEM((ITERS, nrec, cols), BF16),
            pltpu.VMEM((cols, cols), BF16),
            pltpu.VMEM((cols, cols), BF16),
            pltpu.VMEM((ITERS, nrec, QBLOCK), jnp.int32),
            pltpu.VMEM((ITERS, nrec, rows * blocks), F32),
            pltpu.VMEM((nshot, 8, 128), F32),
            pltpu.VMEM((nspace, 8, 128), F32),
            pltpu.VMEM((8, 128), F32),
            pltpu.VMEM((8, 128), F32),
            dma((2, ITERS, NC)),
            dma((2, ITERS, NC)),
            dma((pairs,)),
            dma((pairs,)),
            dma((max(pairs - 1, 1),)),
            dma((max(pairs - 1, 1),)),
            dma((nshot - 1,)),
            dma((nshot - 1,)),
            dma((nspace - 1,)),
            dma((nspace - 1,)),
            dma((8,)),
        ],
        compiler_params=pltpu.CompilerParams(
            collective_id=0, has_side_effects=True, vmem_limit_bytes=66000000
        ),
    )(
        receiver_cell[0],
        source_cell[0],
        scale_table,
        observed[0],
        adjoint_now[0],
        adjoint_later[0],
        courant,
        checkpoint_codes[0],
        scale_index[0],
        receiver_cell,
    )
    count = nshot * ITERS * nrec * nspace
    parts = depth // W
    gradient, first, second, misfit = pl.pallas_call(
        functools.partial(finish, 0.5 / count),
        out_shape=(jax.ShapeDtypeStruct(gradient.shape, F32), field, field, jax.ShapeDtypeStruct((1, 1), F32)),
        in_specs=[anyspace] * 3 + [vmem],
        out_specs=(anyspace, anyspace, anyspace, vmem),
        scratch_shapes=[
            pltpu.VMEM((depth, yq, cols), F32),
            pltpu.VMEM((2 * parts, W, rows, cols), F32),
            dma((2 * parts + 1,)),
            dma((2 * parts + 1,)),
        ],
    )(gradient, first, second, total)
    return (gradient, first[None], second[None], misfit.reshape(()))


def solution(mesh):
    placed = (
        P("shot", "space", None, None),
        P("shot", "space", None, None),
        P("space", None, None),
        P("shot", None, "space", None, None),
        P("shot", None, "space", None),
        P(),
        P("shot", "space"),
        P("shot", None, "space"),
        P("shot", None),
    )
    return jax.shard_map(
        functools.partial(body, mesh.shape["shot"], mesh.shape["space"]),
        mesh=mesh,
        in_specs=placed,
        out_specs=(
            P("space", "shot", None),
            P("shot", "space", None, None),
            P("shot", "space", None, None),
            P(),
        ),
        check_vma=False,
    )
```

profile of v0, /device:TPU:2, one launch (start us, length us, event | category | flops | bytes accessed | tf_op | source)
XLA Modules:
  0.0 110.4 jit_solution(3049685303588755016)
XLA Ops:
  0.6 104.4 %shard_map.120 = (f32[16,16,512]{2,1,0:T(8,128)}, f32[16,64,512]{2,1,0:T(8,128)}, f32[16,64,512]{2,1,0:T(8,128)}, f32[8,128]{1,0:T(8,128)}) custom-call(s32[256]{0:T(256)} %bitcast.15, s32[3]{0:T(128)} %bitcast.16, f32[64]{0:T(128)} %table.1, f32[4,256]{1,0:T(4,128)} %bitcast.14, f32[16,64,512]{2,1,0:T(8,128)} %bitcast.11, f32[16,64,512]{2,1,0:T(8,128)} %bitcast.12, ...), custom_call_target="tpu_custom_call" | custom-call | tf_op jit(solution)/shard_map/pallas_call | solution.py:519
  105.0 5.3 %shard_map.121 = (f32[16,16,512]{2,1,0:T(8,128)}, f32[16,64,512]{2,1,0:T(8,128)}, f32[16,64,512]{2,1,0:T(8,128)}, f32[1,1]{1,0:T(1,128)}) custom-call(f32[16,16,512]{2,1,0:T(8,128)} %get-tuple-element.12.grad, f32[16,64,512]{2,1,0:T(8,128)} %get-tuple-element.13.first, f32[16,64,512]{2,1,0:T(8,128)} %get-tuple-element.14.second, ...), custom_call_target="tpu_custom_call" | custom-call | tf_op jit(solution)/shard_map/pallas_call | solution.py:582
where the time goes:
time: 111 us; the launch traced here: 110 us
  Pallas kernels  110 us (99%)
    pallas_call x1, Pallas kernels, body(): pl.pallas_call(functools.partial(kernel, nshot, nspace), out_shape=(jax.S...  104 us
    pallas_call x1, Pallas kernels, body(): pl.pallas_call(functools.partial(finish, 0.5 / count), out_shape=(jax.Sha...  5.34 us

commit v1 on v0

--- a/solution.py
+++ b/solution.py
@@ -52,8 +52,8 @@
     index,
     cells_row,
     grad,
-    first_h,
-    second_h,
+    first,
+    second,
     misfit,
     E,
     D,
@@ -78,8 +78,11 @@
     SB,
     MT,
     ST,
+    RL,
     halo_send,
     halo_recv,
+    relay_recv,
+    relay_send,
     a_send,
     a_recv,
     b_send,
@@ -111,52 +114,103 @@
             barrier, inc=1, device_id={"space": lax.rem(space + d, nspace)}, device_id_type=MESH
         )
 
-    in_now = pltpu.make_async_copy(now_h, E.at[1, pl.ds(W, depth)], local_sem.at[0])
+    edge_low = pltpu.make_async_copy(
+        now_h.at[pl.ds(0, W)], E.at[1, pl.ds(W, W)], local_sem.at[4]
+    )
+    edge_high = pltpu.make_async_copy(
+        now_h.at[pl.ds(depth - W, W)], E.at[1, pl.ds(depth, W)], local_sem.at[5]
+    )
+    inner = depth - 2 * W
+    in_now = pltpu.make_async_copy(
+        now_h.at[pl.ds(W, inner)], E.at[1, pl.ds(2 * W, inner)], local_sem.at[0]
+    )
     in_later = pltpu.make_async_copy(later_h, E.at[0, pl.ds(W, depth)], local_sem.at[1])
     in_cour = pltpu.make_async_copy(cour_h, cour, local_sem.at[2])
     in_words = pltpu.make_async_copy(words_h, words, local_sem.at[3])
+    edge_low.start()
+    edge_high.start()
     in_words.start()
     in_now.start()
     in_cour.start()
     in_later.start()
 
+    edge_low.wait()
+    edge_high.wait()
     pl.semaphore_wait(barrier, nshot + nspace - 2)
 
-    def halo(t, c, up):
-        ys = pl.ds(c * ych, ych)
-        src_z = W + depth - W if up else W
-        dst_z = 0 if up else W + depth
+    odd = lax.rem(space, 2)
+    column = space // 2
+    columns = nspace // 2
+    lean = W * (columns - 1 - column) // columns
+    full = W * column // columns
+    n_out = jnp.where(odd == 1, lean, full)
+    n_in = jnp.where(odd == 1, full, lean)
+    n_up = odd * n_out
+    n_down = (1 - odd) * n_out
+    most = RL.shape[2]
+
+    def rows_of(c):
+        return pl.ds(c * ych, ych)
+
+    def halo(t, c, p, up):
+        src_z = depth + p if up else W + p
+        dst_z = p if up else W + depth + p
         return pltpu.make_async_remote_copy(
-            src_ref=E.at[t + 1, pl.ds(src_z, W), ys, :],
-            dst_ref=E.at[t + 1, pl.ds(dst_z, W), ys, :],
-            send_sem=halo_send.at[int(up), t, c],
-            recv_sem=halo_recv.at[int(up), t, c],
+            src_ref=E.at[t + 1, src_z, rows_of(c), :],
+            dst_ref=E.at[t + 1, dst_z, rows_of(c), :],
+            send_sem=halo_send.at[int(up), t, c, p],
+            recv_sem=halo_recv.at[int(up), t, c, p],
             device_id={"space": space + (1 if up else -1)},
             device_id_type=MESH,
         )
 
-    def halo_first(c, up):
-        ys = pl.ds(c * ych, ych)
-        src_z = depth - W if up else 0
-        dst_z = 0 if up else W + depth
+    def detour(t, c, p):
         return pltpu.make_async_remote_copy(
-            src_ref=now_h.at[pl.ds(src_z, W), ys, :],
-            dst_ref=E.at[1, pl.ds(dst_z, W), ys, :],
-            send_sem=halo_send.at[int(up), 0, c],
-            recv_sem=halo_recv.at[int(up), 0, c],
-            device_id={"space": space + (1 if up else -1)},
+            src_ref=E.at[t + 1, W + p + odd * (depth - W), rows_of(c), :],
+            dst_ref=RL.at[t, c, p],
+            send_sem=halo_send.at[odd, t, c, p],
+            recv_sem=relay_recv.at[t, c, p],
+            device_id={"space": space + 1 - 2 * odd},
             device_id_type=MESH,
         )
 
+    def onward(t, c, p):
+        return pltpu.make_async_remote_copy(
+            src_ref=RL.at[t, c, p],
+            dst_ref=E.at[t + 1, p + odd * (W + depth), rows_of(c), :],
+            send_sem=relay_send.at[t, c, p],
+            recv_sem=halo_recv.at[1 - odd, t, c, p],
+            device_id={"space": space + 2 - 4 * odd},
+            device_id_type=MESH,
+        )
+
+    def send(t, c):
+        for p in range(most):
+
+            @pl.when(p < n_out)
+            def _():
+                detour(t, c, p).start()
+
+        for p in range(W):
+
+            @pl.when(jnp.logical_and(has_high, p >= n_up))
+            def _():
+                halo(t, c, p, True).start()
+
+            @pl.when(jnp.logical_and(has_low, p >= n_down))
+            def _():
+                halo(t, c, p, False).start()
+
+    def relay(t, c):
+        for p in range(most):
+
+            @pl.when(p < n_in)
+            def _():
+                detour(t, c, p).wait_recv()
+                onward(t, c, p).start()
+
     for c in range(NC):
-
-        @pl.when(has_high)
-        def _():
-            halo_first(c, True).start()
-
-        @pl.when(has_low)
-        def _():
-            halo_first(c, False).start()
+        send(0, c)
 
     @pl.loop(0, cols // 64)
     def _(i):
@@ -240,6 +294,7 @@
     for d in range(1, nshot):
         misfit_copy(d).start()
 
+    relay(0, 0)
     in_now.wait()
     in_later.wait()
     in_cour.wait()
@@ -264,9 +319,7 @@
                 inject = dot(PR[z], QH[t]) + dot(PR[z], QL[t])
                 E[t + 2, W + z] = 2.0 * up - E[t, W + z] + cour[z] * acc + inject
 
-    local(0)
-
-    def decode():
+    def spread():
         i = lax.broadcasted_iota(jnp.int32, (rows, rows * blocks), 0)
         j = lax.broadcasted_iota(jnp.int32, (rows, rows * blocks), 1)
         flat = SC[...].reshape(128, rows * blocks)
@@ -282,8 +335,10 @@
                 )
             TS[m] = moved
 
-        @pl.loop(0, depth)
-        def _(z):
+    def decode(part):
+        @pl.loop(0, depth // 4)
+        def _(step):
+            z = part * (depth // 4) + step
             for m in range(blocks):
                 xs = slice(m * QBLOCK, (m + 1) * QBLOCK)
                 scale = pltpu.roll(TS[m], lax.rem(128 - z, 128), 1)
@@ -299,6 +354,9 @@
                     else:
                         D[t - 1, z, :, xs] = diff
 
+    spread()
+    local(0)
+
     for d in range(1, nshot):
         misfit_copy(d).wait()
     total = MB[0]
@@ -311,122 +369,151 @@
     def _(d):
         total_copy(d).start()
 
-    def fix(t, c):
-        ys = pl.ds(c * ych, ych)
+    def fix(t, c, target, base):
+        ys = rows_of(c)
 
         @pl.when(has_low)
         def _():
-            halo(t, c, True).wait_recv()
+            for p in range(W):
+                halo(t, c, p, True).wait_recv()
             for j in range(W):
                 acc = COEFFS[j + 1] * E[t + 1, W - 1, ys, :]
                 for i in range(j + 2, 5):
                     acc = acc + COEFFS[i] * E[t + 1, W + j - i, ys, :]
-                E[t + 2, W + j, ys, :] += cour[j, ys, :] * acc
+                target[base + j, ys, :] += cour[j, ys, :] * acc
 
         @pl.when(has_high)
         def _():
-            halo(t, c, False).wait_recv()
+            for p in range(W):
+                halo(t, c, p, False).wait_recv()
             for j in range(W):
                 z = depth - 1 - j
                 acc = COEFFS[j + 1] * E[t + 1, W + depth, ys, :]
                 for i in range(j + 2, 5):
                     acc = acc + COEFFS[i] * E[t + 1, W + z + i, ys, :]
-                E[t + 2, W + z, ys, :] += cour[z, ys, :] * acc
-
-    @pl.loop(0, ITERS - 1)
-    def _(t):
-        for c in range(NC):
-            fix(t, c)
-
-            @pl.when(has_high)
-            def _():
-                halo(t + 1, c, True).start()
-
-            @pl.when(has_low)
-            def _():
-                halo(t + 1, c, False).start()
-
-            if c == 0:
-
-                @pl.when(t == 0)
-                def _():
-                    decode()
-
-        local(t + 1)
-
-        @pl.loop(0, depth)
-        def _(z):
-            IM[z] = IM[z] + E[t + 2, W + z] * D[t, z]
-
-    out_second = pltpu.make_async_copy(E.at[ITERS, pl.ds(W, depth)], second_h, local_sem.at[4])
-    out_second.start()
-    inner = depth - 2 * W
-    out_inner = pltpu.make_async_copy(
-        E.at[ITERS + 1, pl.ds(2 * W, inner)], first_h.at[pl.ds(W, inner)], local_sem.at[5]
-    )
-    out_inner.start()
+                target[base + z, ys, :] += cour[z, ys, :] * acc
 
     first_z = space * depth
-
-    @pl.loop(0, depth)
-    def _(z):
+    core = lax.rem(shot, 2)
+    pair = shot // 2
+    pairs = nshot // 2
+    yq = rows // nshot
+    pieces = ((W, inner), (0, W), (depth - W, W))
+
+    def quarter(index):
+        return pl.ds(pl.multiple_of(index * yq, yq), yq)
+
+    def mute(z):
         dz = first_z + z - source_s[0]
         dy = lax.broadcasted_iota(jnp.int32, (rows, cols), 0) - source_s[1]
         dx = lax.broadcasted_iota(jnp.int32, (rows, cols), 1) - source_s[2]
         dist = (dz * dz + dy * dy + dx * dx).astype(F32)
         IM[z] = IM[z] * (1.0 - jnp.exp(dist * (-1.0 / (2.0 * MUTE * MUTE))))
 
-    core = lax.rem(shot, 2)
-    pair = shot // 2
-    pairs = nshot // 2
-    yq = rows // nshot
-
-    def quarter(index):
-        return pl.ds(pl.multiple_of(index * yq, yq), yq)
-
-    def copy_a(h):
+    def copy_a(h, n):
+        at = pl.ds(*pieces[n])
         return pltpu.make_async_remote_copy(
-            src_ref=IM.at[:, quarter(2 * h + 1 - core), :],
-            dst_ref=RA.at[h],
-            send_sem=a_send.at[h],
-            recv_sem=a_recv.at[h],
+            src_ref=IM.at[at, quarter(2 * h + 1 - core), :],
+            dst_ref=RA.at[h, at],
+            send_sem=a_send.at[h, n],
+            recv_sem=a_recv.at[h, n],
             device_id={"shot": shot + 1 - 2 * core},
             device_id_type=MESH,
         )
 
-    def copy_b(d):
-        target = lax.rem(pair + d, pairs)
+    def copy_b(d, n):
+        at = pl.ds(*pieces[n])
+        other = lax.rem(pair + d, pairs)
         return pltpu.make_async_remote_copy(
-            src_ref=S.at[target],
-            dst_ref=RB.at[d - 1],
-            send_sem=b_send.at[d - 1],
-            recv_sem=b_recv.at[d - 1],
-            device_id={"shot": 2 * target + core},
+            src_ref=S.at[other, at],
+            dst_ref=RB.at[d - 1, at],
+            send_sem=b_send.at[d - 1, n],
+            recv_sem=b_recv.at[d - 1, n],
+            device_id={"shot": 2 * other + core},
             device_id_type=MESH,
         )
 
-    for h in range(pairs):
-        copy_a(h).start()
-    for h in range(pairs):
-        copy_a(h).wait()
-        S[h] = IM[:, quarter(2 * h + core), :] + RA[h]
-    for d in range(1, pairs):
-        copy_b(d).start()
-
-    for c in range(NC):
-        fix(ITERS - 1, c)
-    out_low = pltpu.make_async_copy(
-        E.at[ITERS + 1, pl.ds(W, W)], first_h.at[pl.ds(0, W)], local_sem.at[6]
-    )
-    out_high = pltpu.make_async_copy(
-        E.at[ITERS + 1, pl.ds(depth, W)], first_h.at[pl.ds(depth - W, W)], local_sem.at[7]
-    )
-    out_low.start()
-    out_high.start()
+    def offer(n):
+        for h in range(pairs):
+            copy_a(h, n).start()
+
+    def pass_on(n):
+        at = pl.ds(*pieces[n])
+        for h in range(pairs):
+            copy_a(h, n).wait()
+            S[h, at] = IM[at, quarter(2 * h + core), :] + RA[h, at]
+        for d in range(1, pairs):
+            copy_b(d, n).start()
+
+    @pl.loop(0, ITERS - 1)
+    def _(t):
+        fix(t, 0, E.at[t + 2], W)
+        send(t + 1, 0)
+
+        @pl.when(t < 2)
+        def _():
+            decode(2 * t)
+
+        relay(t, 1)
+
+        @pl.when(t < 2)
+        def _():
+            decode(2 * t + 1)
+
+        @pl.when(t == ITERS - 2)
+        def _():
+            pass_on(0)
+
+        fix(t, 1, E.at[t + 2], W)
+        send(t + 1, 1)
+
+        @pl.when(t == ITERS - 2)
+        def _():
+            for low in (0, depth - W):
+
+                @pl.loop(low, low + W)
+                def _(z):
+                    IM[z] = IM[z] + E[ITERS, W + z] * D[ITERS - 2, z]
+                    mute(z)
+
+            offer(1)
+            offer(2)
+
+        local(t + 1)
+        relay(t + 1, 0)
+
+        @pl.when(t == ITERS - 3)
+        def _():
+            @pl.loop(0, depth)
+            def _(z):
+                value = IM[z]
+                for k in range(ITERS - 2):
+                    value = value + E[k + 2, W + z] * D[k, z]
+                IM[z] = value
+
+            @pl.loop(W, depth - W)
+            def _(z):
+                IM[z] = IM[z] + E[ITERS, W + z] * D[ITERS - 2, z]
+                mute(z)
+
+            offer(0)
+
+    pass_on(1)
+    pass_on(2)
+
+    @pl.loop(0, depth)
+    def _(z):
+        second[z] = E[ITERS, W + z]
+        first[z] = E[ITERS + 1, W + z]
+
+    fix(ITERS - 1, 0, first, 0)
+    relay(ITERS - 1, 1)
+    fix(ITERS - 1, 1, first, 0)
 
     total = S[pair]
     for d in range(1, pairs):
-        copy_b(d).wait()
+        for n in range(len(pieces)):
+            copy_b(d, n).wait()
         total = total + RB[d - 1]
     grad[...] = total
 
@@ -439,56 +526,35 @@
         whole = whole + SB[d]
     misfit[...] = whole
 
-    for c in range(NC):
-
-        @pl.when(has_high)
-        def _():
-            halo_first(c, True).wait_send()
-
-        @pl.when(has_low)
-        def _():
-            halo_first(c, False).wait_send()
-
-        @pl.loop(1, ITERS)
-        def _(t):
-            @pl.when(has_high)
-            def _():
-                halo(t, c, True).wait_send()
-
-            @pl.when(has_low)
-            def _():
-                halo(t, c, False).wait_send()
-
-    out_second.wait()
-    out_inner.wait()
-    out_low.wait()
-    out_high.wait()
-
-
-def finish(factor, grad, first, second, total, grad_o, first_o, second_o, misfit, GB, FB, sem_in, sem_out):
-    parts = FB.shape[0] // 2
-    planes = FB.shape[1]
-    moves = []
-    for n, (source, target) in enumerate(((first, first_o), (second, second_o))):
-        for p in range(parts):
-            at = pl.ds(p * planes, planes)
-            moves.append((source.at[at], FB.at[n * parts + p], target.at[at]))
-    moves.append((grad, GB, grad_o))
-    into = [
-        pltpu.make_async_copy(source, held, sem_in.at[n])
-        for n, (source, held, target) in enumerate(moves)
+    @pl.loop(0, ITERS)
+    def _(t):
+        for c in range(NC):
+            for p in range(W):
+
+                @pl.when(has_high)
+                def _():
+                    halo(t, c, p, True).wait_send()
+
+                @pl.when(has_low)
+                def _():
+                    halo(t, c, p, False).wait_send()
+
+            for p in range(most):
+
+                @pl.when(p < n_in)
+                def _():
+                    onward(t, c, p).wait_send()
+
+
+def finish(factor, grad, first, second, total, grad_o, first_o, second_o, misfit, sem):
+    copies = [
+        pltpu.make_async_copy(source, target, sem.at[n])
+        for n, (source, target) in enumerate(((first, first_o), (second, second_o), (grad, grad_o)))
     ]
-    out = [
-        pltpu.make_async_copy(held, target, sem_out.at[n])
-        for n, (source, held, target) in enumerate(moves)
-    ]
-    for copy in into:
+    for copy in copies:
         copy.start()
     misfit[...] = total[0:1, 0:1] * factor
-    for n in range(len(moves)):
-        into[n].wait()
-        out[n].start()
-    for copy in out:
+    for copy in copies:
         copy.wait()
 
 
@@ -513,19 +579,22 @@
     yq = rows // nshot
     vmem = pl.BlockSpec(memory_space=pltpu.VMEM)
     smem = pl.BlockSpec(memory_space=pltpu.SMEM)
-    anyspace = pl.BlockSpec(memory_space=pl.ANY)
+    anyspace = pl.BlockSpec(memory_space=pltpu.HBM)
     dma = pltpu.SemaphoreType.DMA
+    held = pltpu.VMEM((depth, rows, cols), F32)
     field = jax.ShapeDtypeStruct((depth, rows, cols), F32)
+    columns = nspace // 2
+    most = max(W * (columns - 1) // columns, 1)
     gradient, first, second, total = pl.pallas_call(
         functools.partial(kernel, nshot, nspace),
         out_shape=(
-            jax.ShapeDtypeStruct((depth, yq, cols), F32),
-            field,
-            field,
-            jax.ShapeDtypeStruct((8, 128), F32),
+            pltpu.VMEM((depth, yq, cols), F32),
+            held,
+            held,
+            pltpu.VMEM((8, 128), F32),
         ),
         in_specs=[smem] * 4 + [anyspace] * 4 + [vmem] * 2,
-        out_specs=(vmem, anyspace, anyspace, vmem),
+        out_specs=(vmem, vmem, vmem, vmem),
         scratch_shapes=[
             pltpu.VMEM((ITERS + 2, depth + 2 * W, rows, cols), F32),
             pltpu.VMEM((ITERS - 1, depth, rows, cols), F32),
@@ -550,20 +619,23 @@
             pltpu.VMEM((nspace, 8, 128), F32),
             pltpu.VMEM((8, 128), F32),
             pltpu.VMEM((8, 128), F32),
-            dma((2, ITERS, NC)),
-            dma((2, ITERS, NC)),
-            dma((pairs,)),
-            dma((pairs,)),
-            dma((max(pairs - 1, 1),)),
-            dma((max(pairs - 1, 1),)),
+            pltpu.VMEM((ITERS, NC, most, rows // NC, cols), F32),
+            dma((2, ITERS, NC, W)),
+            dma((2, ITERS, NC, W)),
+            dma((ITERS, NC, most)),
+            dma((ITERS, NC, most)),
+            dma((pairs, 3)),
+            dma((pairs, 3)),
+            dma((max(pairs - 1, 1), 3)),
+            dma((max(pairs - 1, 1), 3)),
             dma((nshot - 1,)),
             dma((nshot - 1,)),
             dma((nspace - 1,)),
             dma((nspace - 1,)),
-            dma((8,)),
+            dma((6,)),
         ],
         compiler_params=pltpu.CompilerParams(
-            collective_id=0, has_side_effects=True, vmem_limit_bytes=66000000
+            collective_id=0, has_side_effects=True, vmem_limit_bytes=52000000
         ),
     )(
         receiver_cell[0],
@@ -578,18 +650,13 @@
         receiver_cell,
     )
     count = nshot * ITERS * nrec * nspace
-    parts = depth // W
     gradient, first, second, misfit = pl.pallas_call(
         functools.partial(finish, 0.5 / count),
         out_shape=(jax.ShapeDtypeStruct(gradient.shape, F32), field, field, jax.ShapeDtypeStruct((1, 1), F32)),
-        in_specs=[anyspace] * 3 + [vmem],
+        in_specs=[vmem] * 4,
         out_specs=(anyspace, anyspace, anyspace, vmem),
-        scratch_shapes=[
-            pltpu.VMEM((depth, yq, cols), F32),
-            pltpu.VMEM((2 * parts, W, rows, cols), F32),
-            dma((2 * parts + 1,)),
-            dma((2 * parts + 1,)),
-        ],
+        scratch_shapes=[dma((3,))],
+        compiler_params=pltpu.CompilerParams(vmem_limit_bytes=16000000),
     )(gradient, first, second, total)
     return (gradient, first[None], second[None], misfit.reshape(()))
 

time: 111 us -> 93.8 us (0.85)
  the two profiles are of different devices: /device:TPU:2 before, /device:TPU:0 now
where the time goes in v1:
time: 93.8 us; the launch traced here: 93.7 us
  Pallas kernels  93 us (99%)
    pallas_call x1, Pallas kernels, body(): pl.pallas_call(functools.partial(kernel, nshot, nspace), out_shape=(pltpu...  90.3 us
    pallas_call x1, Pallas kernels, body(): pl.pallas_call(functools.partial(finish, 0.5 / count), out_shape=(jax.Sha...  2.71 us

profile of v1, /device:TPU:0, one launch (start us, length us, event | category | flops | bytes accessed | tf_op | source)
XLA Modules:
  0.0 93.7 jit_solution(8952003824269370870)
XLA Ops:
  0.6 90.3 %shard_map.120 = (f32[16,16,512]{2,1,0:T(8,128)S(1)}, f32[16,64,512]{2,1,0:T(8,128)S(1)}, f32[16,64,512]{2,1,0:T(8,128)S(1)}, f32[8,128]{1,0:T(8,128)S(1)}) custom-call(s32[256]{0:T(256)} %bitcast.15, s32[3]{0:T(128)} %bitcast.16, f32[64]{0:T(128)} %table.1, f32[4,256]{1,0:T(4,128)} %bitcast.14, f32[16,64,512]{2,1,0:T(8,128)} %bitcast.11, ...), custom_call_target="tpu_custom_call" | custom-call | tf_op jit(solution)/shard_map/pallas_call | solution.py:588
  90.9 2.7 %shard_map.121 = (f32[16,16,512]{2,1,0:T(8,128)}, f32[16,64,512]{2,1,0:T(8,128)}, f32[16,64,512]{2,1,0:T(8,128)}, f32[1,1]{1,0:T(1,128)}) custom-call(f32[16,16,512]{2,1,0:T(8,128)S(1)} %get-tuple-element.12.grad, f32[16,64,512]{2,1,0:T(8,128)S(1)} %get-tuple-element.13.first, f32[16,64,512]{2,1,0:T(8,128)S(1)} %get-tuple-element.14.second, ...), custom_call_target="tpu_custom_call" | custom-call | tf_op jit(solution)/shard_map/pallas_call | solution.py:653

commit v2 on v1

--- a/solution.py
+++ b/solution.py
@@ -41,20 +41,25 @@
 def kernel(
     nshot,
     nspace,
+    cells_h,
+    source_h,
+    table_h,
+    observed_h,
+    now_h,
+    later_h,
+    cour_h,
+    words_h,
+    index_h,
+    grad,
+    first,
+    second,
+    misfit,
     cells_s,
     source_s,
     table,
     observed,
-    now_h,
-    later_h,
-    cour_h,
-    words_h,
     index,
     cells_row,
-    grad,
-    first,
-    second,
-    misfit,
     E,
     D,
     cour,
@@ -75,9 +80,11 @@
     GW,
     GS,
     MB,
-    SB,
     MT,
     ST,
+    PX,
+    CO,
+    CI,
     RL,
     halo_send,
     halo_recv,
@@ -89,8 +96,10 @@
     b_recv,
     m_send,
     m_recv,
+    p_sem,
     s_send,
     s_recv,
+    small_sem,
     local_sem,
 ):
     depth, rows, cols = cour.shape
@@ -108,11 +117,14 @@
             barrier, inc=1, device_id={"shot": lax.rem(shot + d, nshot)}, device_id_type=MESH
         )
 
-    @pl.loop(1, nspace)
-    def _(d):
-        pl.semaphore_signal(
-            barrier, inc=1, device_id={"space": lax.rem(space + d, nspace)}, device_id_type=MESH
-        )
+    near = ((-2, space >= 2), (-1, has_low), (1, has_high), (2, space < nspace - 2))
+    for d, there in near:
+
+        @pl.when(there)
+        def _():
+            pl.semaphore_signal(
+                barrier, inc=1, device_id={"space": space + d}, device_id_type=MESH
+            )
 
     edge_low = pltpu.make_async_copy(
         now_h.at[pl.ds(0, W)], E.at[1, pl.ds(W, W)], local_sem.at[4]
@@ -133,10 +145,26 @@
     in_now.start()
     in_cour.start()
     in_later.start()
+    small = [
+        pltpu.make_async_copy(source, target, small_sem.at[n])
+        for n, (source, target) in enumerate(
+            (
+                (index_h, index),
+                (cells_h, cells_row),
+                (cells_h, cells_s),
+                (source_h, source_s),
+                (table_h, table),
+                (observed_h, observed),
+            )
+        )
+    ]
+    for copy in small:
+        copy.start()
 
     edge_low.wait()
     edge_high.wait()
-    pl.semaphore_wait(barrier, nshot + nspace - 2)
+    present = sum(there.astype(jnp.int32) for _, there in near)
+    pl.semaphore_wait(barrier, nshot - 1 + present)
 
     odd = lax.rem(space, 2)
     column = space // 2
@@ -152,14 +180,14 @@
     def rows_of(c):
         return pl.ds(c * ych, ych)
 
-    def halo(t, c, p, up):
+    def halo(t, c, p, up, planes=1):
         src_z = depth + p if up else W + p
         dst_z = p if up else W + depth + p
         return pltpu.make_async_remote_copy(
-            src_ref=E.at[t + 1, src_z, rows_of(c), :],
-            dst_ref=E.at[t + 1, dst_z, rows_of(c), :],
-            send_sem=halo_send.at[int(up), t, c, p],
-            recv_sem=halo_recv.at[int(up), t, c, p],
+            src_ref=E.at[t + 1, pl.ds(src_z, planes), rows_of(c), :],
+            dst_ref=E.at[t + 1, pl.ds(dst_z, planes), rows_of(c), :],
+            send_sem=halo_send.at[int(up), t, c],
+            recv_sem=halo_recv.at[int(up), t, c],
             device_id={"space": space + (1 if up else -1)},
             device_id_type=MESH,
         )
@@ -168,7 +196,7 @@
         return pltpu.make_async_remote_copy(
             src_ref=E.at[t + 1, W + p + odd * (depth - W), rows_of(c), :],
             dst_ref=RL.at[t, c, p],
-            send_sem=halo_send.at[odd, t, c, p],
+            send_sem=halo_send.at[odd, t, c],
             recv_sem=relay_recv.at[t, c, p],
             device_id={"space": space + 1 - 2 * odd},
             device_id_type=MESH,
@@ -179,7 +207,7 @@
             src_ref=RL.at[t, c, p],
             dst_ref=E.at[t + 1, p + odd * (W + depth), rows_of(c), :],
             send_sem=relay_send.at[t, c, p],
-            recv_sem=halo_recv.at[1 - odd, t, c, p],
+            recv_sem=halo_recv.at[1 - odd, t, c],
             device_id={"space": space + 2 - 4 * odd},
             device_id_type=MESH,
         )
@@ -208,6 +236,21 @@
             def _():
                 detour(t, c, p).wait_recv()
                 onward(t, c, p).start()
+
+    def drain(t, c):
+        @pl.when(has_high)
+        def _():
+            halo(t, c, 0, True, W).wait_send()
+
+        @pl.when(has_low)
+        def _():
+            halo(t, c, 0, False, W).wait_send()
+
+        for p in range(most):
+
+            @pl.when(p < n_in)
+            def _():
+                onward(t, c, p).wait_send()
 
     for c in range(NC):
         send(0, c)
@@ -220,6 +263,8 @@
         CL[pl.ds(start, 64), :] = low
 
     yh, yl = band(rows, rows, 0)
+    for copy in small:
+        copy.wait()
 
     entry = index[...]
     scale = jnp.zeros(entry.shape, F32)
@@ -234,7 +279,7 @@
 
     @pl.loop(0, nrec, unroll=4)
     def _(r):
-        cell = lax.rem(cells_s[r], slab)
+        cell = lax.rem(cells_s[0, r], slab)
         row = cell // cols
         z = row // rows
         y = lax.rem(row, rows)
@@ -281,15 +326,43 @@
             device_id_type=MESH,
         )
 
-    def total_copy(d):
+    def pair_copy():
         return pltpu.make_async_remote_copy(
             src_ref=ST,
-            dst_ref=SB.at[space],
-            send_sem=s_send.at[d - 1],
-            recv_sem=s_recv.at[d - 1],
-            device_id={"space": lax.rem(space + d, nspace)},
+            dst_ref=PX,
+            send_sem=p_sem.at[0],
+            recv_sem=p_sem.at[1],
+            device_id={"space": space + 1 - 2 * odd},
             device_id_type=MESH,
         )
+
+    def chain_copy(way):
+        return pltpu.make_async_remote_copy(
+            src_ref=CO.at[way],
+            dst_ref=CI.at[way],
+            send_sem=s_send.at[way],
+            recv_sem=s_recv.at[way],
+            device_id={"space": space + (2 if way else -2)},
+            device_id_type=MESH,
+        )
+
+    def chain(slot):
+        for way in (0, 1):
+            place = column if way else columns - 1 - column
+            turn = jnp.logical_or(place == slot, jnp.logical_and(slot == 3, place > slot))
+
+            @pl.when(turn)
+            def _():
+                @pl.when(place > 0)
+                def _():
+                    chain_copy(way).wait_recv()
+                    CO[way] = CI[way]
+
+                CO[way, pl.ds(column, 1)] = (ST[...] + PX[...]).reshape(1, 8, 128)
+
+                @pl.when(place < columns - 1)
+                def _():
+                    chain_copy(way).start()
 
     for d in range(1, nshot):
         misfit_copy(d).start()
@@ -299,8 +372,10 @@
     in_later.wait()
     in_cour.wait()
 
-    def local(t):
-        for g in (0, depth // W - 1) + tuple(range(1, depth // W - 1)):
+    groups = (0, depth // W - 1) + tuple(range(1, depth // W - 1))
+
+    def local(t, chosen):
+        for g in chosen:
             z0 = g * W
             u = E[t + 1, W + z0 : W + z0 + W].reshape(W * rows, cols)
             uh, ul = split(u)
@@ -355,7 +430,7 @@
                         D[t - 1, z, :, xs] = diff
 
     spread()
-    local(0)
+    local(0, groups)
 
     for d in range(1, nshot):
         misfit_copy(d).wait()
@@ -363,19 +438,15 @@
     for d in range(1, nshot):
         total = total + MB[d]
     ST[...] = total
-    SB[pl.ds(space, 1)] = total.reshape(1, 8, 128)
-
-    @pl.loop(1, nspace)
-    def _(d):
-        total_copy(d).start()
+    pair_copy().start()
+    CO[...] = jnp.zeros(CO.shape, F32)
 
     def fix(t, c, target, base):
         ys = rows_of(c)
 
         @pl.when(has_low)
         def _():
-            for p in range(W):
-                halo(t, c, p, True).wait_recv()
+            halo(t, c, 0, True, W).wait_recv()
             for j in range(W):
                 acc = COEFFS[j + 1] * E[t + 1, W - 1, ys, :]
                 for i in range(j + 2, 5):
@@ -384,8 +455,7 @@
 
         @pl.when(has_high)
         def _():
-            for p in range(W):
-                halo(t, c, p, False).wait_recv()
+            halo(t, c, 0, False, W).wait_recv()
             for j in range(W):
                 z = depth - 1 - j
                 acc = COEFFS[j + 1] * E[t + 1, W + depth, ys, :]
@@ -404,9 +474,9 @@
         return pl.ds(pl.multiple_of(index * yq, yq), yq)
 
     def mute(z):
-        dz = first_z + z - source_s[0]
-        dy = lax.broadcasted_iota(jnp.int32, (rows, cols), 0) - source_s[1]
-        dx = lax.broadcasted_iota(jnp.int32, (rows, cols), 1) - source_s[2]
+        dz = first_z + z - source_s[0, 0]
+        dy = lax.broadcasted_iota(jnp.int32, (rows, cols), 0) - source_s[0, 1]
+        dx = lax.broadcasted_iota(jnp.int32, (rows, cols), 1) - source_s[0, 2]
         dist = (dz * dz + dy * dy + dx * dx).astype(F32)
         IM[z] = IM[z] * (1.0 - jnp.exp(dist * (-1.0 / (2.0 * MUTE * MUTE))))
 
@@ -450,6 +520,14 @@
         fix(t, 0, E.at[t + 2], W)
         send(t + 1, 0)
 
+        @pl.when(t == 1)
+        def _():
+            pair_copy().wait()
+
+        @pl.when(t > 0)
+        def _():
+            chain(2 * t - 2)
+
         @pl.when(t < 2)
         def _():
             decode(2 * t)
@@ -479,8 +557,22 @@
             offer(1)
             offer(2)
 
-        local(t + 1)
+        local(t + 1, groups[:2])
         relay(t + 1, 0)
+
+        @pl.when(t == ITERS - 2)
+        def _():
+            pass_on(1)
+            pass_on(2)
+
+        local(t + 1, groups[2:])
+
+        @pl.when(t > 0)
+        def _():
+            chain(2 * t - 1)
+
+        drain(t, 0)
+        drain(t, 1)
 
         @pl.when(t == ITERS - 3)
         def _():
@@ -498,9 +590,6 @@
 
             offer(0)
 
-    pass_on(1)
-    pass_on(2)
-
     @pl.loop(0, depth)
     def _(z):
         second[z] = E[ITERS, W + z]
@@ -508,6 +597,7 @@
 
     fix(ITERS - 1, 0, first, 0)
     relay(ITERS - 1, 1)
+    drain(ITERS - 1, 0)
     fix(ITERS - 1, 1, first, 0)
 
     total = S[pair]
@@ -517,33 +607,21 @@
         total = total + RB[d - 1]
     grad[...] = total
 
-    @pl.loop(1, nspace)
-    def _(d):
-        total_copy(d).wait()
-
-    whole = SB[0]
-    for d in range(1, nspace):
-        whole = whole + SB[d]
+    whole = jnp.zeros((8, 128), F32)
+    for way in (0, 1):
+        @pl.when(column != (columns - 1 if way else 0))
+        def _():
+            chain_copy(way).wait_send()
+
+    @pl.when(column < columns - 1)
+    def _():
+        CO[1] = CO[1] + CI[0]
+
+    for k in range(columns):
+        whole = whole + CO[1, k]
     misfit[...] = whole
 
-    @pl.loop(0, ITERS)
-    def _(t):
-        for c in range(NC):
-            for p in range(W):
-
-                @pl.when(has_high)
-                def _():
-                    halo(t, c, p, True).wait_send()
-
-                @pl.when(has_low)
-                def _():
-                    halo(t, c, p, False).wait_send()
-
-            for p in range(most):
-
-                @pl.when(p < n_in)
-                def _():
-                    onward(t, c, p).wait_send()
+    drain(ITERS - 1, 1)
 
 
 def finish(factor, grad, first, second, total, grad_o, first_o, second_o, misfit, sem):
@@ -578,7 +656,6 @@
     pairs = nshot // 2
     yq = rows // nshot
     vmem = pl.BlockSpec(memory_space=pltpu.VMEM)
-    smem = pl.BlockSpec(memory_space=pltpu.SMEM)
     anyspace = pl.BlockSpec(memory_space=pltpu.HBM)
     dma = pltpu.SemaphoreType.DMA
     held = pltpu.VMEM((depth, rows, cols), F32)
@@ -593,9 +670,15 @@
             held,
             pltpu.VMEM((8, 128), F32),
         ),
-        in_specs=[smem] * 4 + [anyspace] * 4 + [vmem] * 2,
+        in_specs=[anyspace] * 9,
         out_specs=(vmem, vmem, vmem, vmem),
         scratch_shapes=[
+            pltpu.SMEM(receiver_cell.shape, jnp.int32),
+            pltpu.SMEM(source_cell.shape, jnp.int32),
+            pltpu.SMEM(scale_table.shape, F32),
+            pltpu.SMEM(observed.shape[1:], F32),
+            pltpu.VMEM(scale_index.shape[1:], jnp.int32),
+            pltpu.VMEM(receiver_cell.shape, jnp.int32),
             pltpu.VMEM((ITERS + 2, depth + 2 * W, rows, cols), F32),
             pltpu.VMEM((ITERS - 1, depth, rows, cols), F32),
             pltpu.VMEM((depth, rows, cols), F32),
@@ -616,12 +699,14 @@
             pltpu.VMEM((ITERS, nrec, QBLOCK), jnp.int32),
             pltpu.VMEM((ITERS, nrec, rows * blocks), F32),
             pltpu.VMEM((nshot, 8, 128), F32),
-            pltpu.VMEM((nspace, 8, 128), F32),
             pltpu.VMEM((8, 128), F32),
             pltpu.VMEM((8, 128), F32),
+            pltpu.VMEM((8, 128), F32),
+            pltpu.VMEM((2, columns, 8, 128), F32),
+            pltpu.VMEM((2, columns, 8, 128), F32),
             pltpu.VMEM((ITERS, NC, most, rows // NC, cols), F32),
-            dma((2, ITERS, NC, W)),
-            dma((2, ITERS, NC, W)),
+            dma((2, ITERS, NC)),
+            dma((2, ITERS, NC)),
             dma((ITERS, NC, most)),
             dma((ITERS, NC, most)),
             dma((pairs, 3)),
@@ -630,16 +715,18 @@
             dma((max(pairs - 1, 1), 3)),
             dma((nshot - 1,)),
             dma((nshot - 1,)),
-            dma((nspace - 1,)),
-            dma((nspace - 1,)),
+            dma((2,)),
+            dma((2,)),
+            dma((2,)),
+            dma((6,)),
             dma((6,)),
         ],
         compiler_params=pltpu.CompilerParams(
             collective_id=0, has_side_effects=True, vmem_limit_bytes=52000000
         ),
     )(
-        receiver_cell[0],
-        source_cell[0],
+        receiver_cell,
+        source_cell,
         scale_table,
         observed[0],
         adjoint_now[0],
@@ -647,7 +734,6 @@
         courant,
         checkpoint_codes[0],
         scale_index[0],
-        receiver_cell,
     )
     count = nshot * ITERS * nrec * nspace
     gradient, first, second, misfit = pl.pallas_call(

time: 93.8 us -> 89 us (0.949)
  Pallas kernels: 93 us -> 88.2 us
    pallas_call x1, Pallas kernels: 90.3 us -> 85.5 us  [body(): pl.pallas_call(functools.partial(kernel, nshot, nspace), out_shape=(pltpu...]
where the time goes in v2:
time: 89 us; the launch traced here: 88.9 us
  Pallas kernels  88.2 us (99%)
    pallas_call x1, Pallas kernels, body(): pl.pallas_call(functools.partial(kernel, nshot, nspace), out_shape=(pltpu...  85.5 us
    pallas_call x1, Pallas kernels, body(): pl.pallas_call(functools.partial(finish, 0.5 / count), out_shape=(jax.Sha...  2.71 us

profile of v2, /device:TPU:0, one launch (start us, length us, event | category | flops | bytes accessed | tf_op | source)
XLA Modules:
  0.0 88.9 jit_solution(14341393149511231139)
XLA Ops:
  0.6 85.5 %shard_map.120 = (f32[16,16,512]{2,1,0:T(8,128)S(1)}, f32[16,64,512]{2,1,0:T(8,128)S(1)}, f32[16,64,512]{2,1,0:T(8,128)S(1)}, f32[8,128]{1,0:T(8,128)S(1)}) custom-call(s32[1,256]{1,0:T(1,128)} %cells_h.1, s32[1,3]{1,0:T(1,128)} %source_h.1, f32[64]{0:T(128)} %table_h.1, f32[4,256]{1,0:T(4,128)} %bitcast.12, f32[16,64,512]{2,1,0:T(8,128)} %bitcast.9, ...), custom_call_target="tpu_custom_call" | custom-call | tf_op jit(solution)/shard_map/pallas_call | solution.py:665
  86.1 2.7 %shard_map.121 = (f32[16,16,512]{2,1,0:T(8,128)}, f32[16,64,512]{2,1,0:T(8,128)}, f32[16,64,512]{2,1,0:T(8,128)}, f32[1,1]{1,0:T(1,128)}) custom-call(f32[16,16,512]{2,1,0:T(8,128)S(1)} %get-tuple-element.12.grad, f32[16,64,512]{2,1,0:T(8,128)S(1)} %get-tuple-element.13.first, f32[16,64,512]{2,1,0:T(8,128)S(1)} %get-tuple-element.14.second, ...), custom_call_target="tpu_custom_call" | custom-call | tf_op jit(solution)/shard_map/pallas_call | solution.py:739

commit v3 on v2

--- a/solution.py
+++ b/solution.py
@@ -94,8 +94,7 @@
     a_recv,
     b_send,
     b_recv,
-    m_send,
-    m_recv,
+    m_sem,
     p_sem,
     s_send,
     s_recv,
@@ -112,25 +111,25 @@
     has_high = space < nspace - 1
 
     barrier = pltpu.get_barrier_semaphore()
+    near = ((-2, space >= 2), (-1, has_low), (1, has_high), (2, space < nspace - 2))
+    for d, there in near:
+
+        @pl.when(there)
+        def _():
+            pl.semaphore_signal(
+                barrier, inc=1, device_id={"space": space + d}, device_id_type=MESH
+            )
+
     for d in range(1, nshot):
         pl.semaphore_signal(
             barrier, inc=1, device_id={"shot": lax.rem(shot + d, nshot)}, device_id_type=MESH
         )
-
-    near = ((-2, space >= 2), (-1, has_low), (1, has_high), (2, space < nspace - 2))
-    for d, there in near:
-
-        @pl.when(there)
-        def _():
-            pl.semaphore_signal(
-                barrier, inc=1, device_id={"space": space + d}, device_id_type=MESH
-            )
 
     edge_low = pltpu.make_async_copy(
         now_h.at[pl.ds(0, W)], E.at[1, pl.ds(W, W)], local_sem.at[4]
     )
     edge_high = pltpu.make_async_copy(
-        now_h.at[pl.ds(depth - W, W)], E.at[1, pl.ds(depth, W)], local_sem.at[5]
+        now_h.at[pl.ds(depth - W, W)], E.at[1, pl.ds(depth, W)], local_sem.at[4]
     )
     inner = depth - 2 * W
     in_now = pltpu.make_async_copy(
@@ -161,8 +160,9 @@
     for copy in small:
         copy.start()
 
-    edge_low.wait()
-    edge_high.wait()
+    pltpu.make_async_copy(
+        now_h.at[pl.ds(0, 2 * W)], E.at[1, pl.ds(W, 2 * W)], local_sem.at[4]
+    ).wait()
     present = sum(there.astype(jnp.int32) for _, there in near)
     pl.semaphore_wait(barrier, nshot - 1 + present)
 
@@ -173,8 +173,14 @@
     full = W * column // columns
     n_out = jnp.where(odd == 1, lean, full)
     n_in = jnp.where(odd == 1, full, lean)
-    n_up = odd * n_out
-    n_down = (1 - odd) * n_out
+
+    def eased(count, side, t, c):
+        if c != NC - 1:
+            return count
+        early = jnp.logical_and(odd == side, jnp.logical_and(column == 0, lax.rem(shot, 2) == 0))
+        early = jnp.logical_and(early, t == ITERS - 1)
+        return jnp.where(early, jnp.maximum(count - 1, 0), count)
+
     most = RL.shape[2]
 
     def rows_of(c):
@@ -186,8 +192,8 @@
         return pltpu.make_async_remote_copy(
             src_ref=E.at[t + 1, pl.ds(src_z, planes), rows_of(c), :],
             dst_ref=E.at[t + 1, pl.ds(dst_z, planes), rows_of(c), :],
-            send_sem=halo_send.at[int(up), t, c],
-            recv_sem=halo_recv.at[int(up), t, c],
+            send_sem=halo_send.at[int(up), t % 2, c],
+            recv_sem=halo_recv.at[int(up), t % 2, c],
             device_id={"space": space + (1 if up else -1)},
             device_id_type=MESH,
         )
@@ -196,43 +202,45 @@
         return pltpu.make_async_remote_copy(
             src_ref=E.at[t + 1, W + p + odd * (depth - W), rows_of(c), :],
             dst_ref=RL.at[t, c, p],
-            send_sem=halo_send.at[odd, t, c],
-            recv_sem=relay_recv.at[t, c, p],
+            send_sem=halo_send.at[odd, t % 2, c],
+            recv_sem=relay_recv.at[t % 2, c, p],
             device_id={"space": space + 1 - 2 * odd},
             device_id_type=MESH,
         )
 
-    def onward(t, c, p):
+    def onward(t, c, p, planes=1):
         return pltpu.make_async_remote_copy(
-            src_ref=RL.at[t, c, p],
-            dst_ref=E.at[t + 1, p + odd * (W + depth), rows_of(c), :],
-            send_sem=relay_send.at[t, c, p],
-            recv_sem=halo_recv.at[1 - odd, t, c],
+            src_ref=RL.at[t, c, pl.ds(p, planes)],
+            dst_ref=E.at[t + 1, pl.ds(p + odd * (W + depth), planes), rows_of(c), :],
+            send_sem=relay_send.at[t % 2, c],
+            recv_sem=halo_recv.at[1 - odd, t % 2, c],
             device_id={"space": space + 2 - 4 * odd},
             device_id_type=MESH,
         )
 
     def send(t, c):
+        out = eased(n_out, 1, t, c)
         for p in range(most):
 
-            @pl.when(p < n_out)
+            @pl.when(p < out)
             def _():
                 detour(t, c, p).start()
 
         for p in range(W):
 
-            @pl.when(jnp.logical_and(has_high, p >= n_up))
+            @pl.when(jnp.logical_and(has_high, p >= odd * out))
             def _():
                 halo(t, c, p, True).start()
 
-            @pl.when(jnp.logical_and(has_low, p >= n_down))
+            @pl.when(jnp.logical_and(has_low, p >= (1 - odd) * out))
             def _():
                 halo(t, c, p, False).start()
 
     def relay(t, c):
+        n = eased(n_in, 0, t, c)
         for p in range(most):
 
-            @pl.when(p < n_in)
+            @pl.when(p < n)
             def _():
                 detour(t, c, p).wait_recv()
                 onward(t, c, p).start()
@@ -246,11 +254,12 @@
         def _():
             halo(t, c, 0, False, W).wait_send()
 
-        for p in range(most):
-
-            @pl.when(p < n_in)
+        n = eased(n_in, 0, t, c)
+        for count in range(1, most + 1):
+
+            @pl.when(n == count)
             def _():
-                onward(t, c, p).wait_send()
+                onward(t, c, 0, count).wait_send()
 
     for c in range(NC):
         send(0, c)
@@ -320,8 +329,8 @@
         return pltpu.make_async_remote_copy(
             src_ref=MT,
             dst_ref=MB.at[shot],
-            send_sem=m_send.at[d - 1],
-            recv_sem=m_recv.at[d - 1],
+            send_sem=m_sem.at[0],
+            recv_sem=m_sem.at[1],
             device_id={"shot": lax.rem(shot + d, nshot)},
             device_id_type=MESH,
         )
@@ -432,8 +441,14 @@
     spread()
     local(0, groups)
 
-    for d in range(1, nshot):
-        misfit_copy(d).wait()
+    pltpu.make_async_remote_copy(
+        src_ref=MB.at[pl.ds(0, nshot - 1)],
+        dst_ref=MB.at[pl.ds(0, nshot - 1)],
+        send_sem=m_sem.at[0],
+        recv_sem=m_sem.at[1],
+        device_id={"shot": lax.rem(shot + 1, nshot)},
+        device_id_type=MESH,
+    ).wait()
     total = MB[0]
     for d in range(1, nshot):
         total = total + MB[d]
@@ -468,7 +483,7 @@
     pair = shot // 2
     pairs = nshot // 2
     yq = rows // nshot
-    pieces = ((W, inner), (0, W), (depth - W, W))
+    pieces = (((W, inner),), ((0, W), (depth - W, W)))
 
     def quarter(index):
         return pl.ds(pl.multiple_of(index * yq, yq), yq)
@@ -480,19 +495,17 @@
         dist = (dz * dz + dy * dy + dx * dx).astype(F32)
         IM[z] = IM[z] * (1.0 - jnp.exp(dist * (-1.0 / (2.0 * MUTE * MUTE))))
 
-    def copy_a(h, n):
-        at = pl.ds(*pieces[n])
+    def copy_a(source, target, n):
         return pltpu.make_async_remote_copy(
-            src_ref=IM.at[at, quarter(2 * h + 1 - core), :],
-            dst_ref=RA.at[h, at],
-            send_sem=a_send.at[h, n],
-            recv_sem=a_recv.at[h, n],
+            src_ref=source,
+            dst_ref=target,
+            send_sem=a_send.at[n],
+            recv_sem=a_recv.at[n],
             device_id={"shot": shot + 1 - 2 * core},
             device_id_type=MESH,
         )
 
-    def copy_b(d, n):
-        at = pl.ds(*pieces[n])
+    def copy_b(d, n, at):
         other = lax.rem(pair + d, pairs)
         return pltpu.make_async_remote_copy(
             src_ref=S.at[other, at],
@@ -503,17 +516,23 @@
             device_id_type=MESH,
         )
 
+    def whole_of(n):
+        return pl.ds(0, sum(count for _, count in pieces[n]))
+
     def offer(n):
-        for h in range(pairs):
-            copy_a(h, n).start()
+        for piece in pieces[n]:
+            at = pl.ds(*piece)
+            for h in range(pairs):
+                copy_a(IM.at[at, quarter(2 * h + 1 - core), :], RA.at[h, at], n).start()
 
     def pass_on(n):
-        at = pl.ds(*pieces[n])
-        for h in range(pairs):
-            copy_a(h, n).wait()
-            S[h, at] = IM[at, quarter(2 * h + core), :] + RA[h, at]
-        for d in range(1, pairs):
-            copy_b(d, n).start()
+        copy_a(S.at[:, whole_of(n)], RA.at[:, whole_of(n)], n).wait()
+        for piece in pieces[n]:
+            at = pl.ds(*piece)
+            for h in range(pairs):
+                S[h, at] = IM[at, quarter(2 * h + core), :] + RA[h, at]
+            for d in range(1, pairs):
+                copy_b(d, n, at).start()
 
     @pl.loop(0, ITERS - 1)
     def _(t):
@@ -555,7 +574,6 @@
                     mute(z)
 
             offer(1)
-            offer(2)
 
         local(t + 1, groups[:2])
         relay(t + 1, 0)
@@ -563,7 +581,6 @@
         @pl.when(t == ITERS - 2)
         def _():
             pass_on(1)
-            pass_on(2)
 
         local(t + 1, groups[2:])
 
@@ -598,12 +615,10 @@
     fix(ITERS - 1, 0, first, 0)
     relay(ITERS - 1, 1)
     drain(ITERS - 1, 0)
-    fix(ITERS - 1, 1, first, 0)
-
     total = S[pair]
     for d in range(1, pairs):
         for n in range(len(pieces)):
-            copy_b(d, n).wait()
+            copy_b(d, n, whole_of(n)).wait()
         total = total + RB[d - 1]
     grad[...] = total
 
@@ -620,6 +635,8 @@
     for k in range(columns):
         whole = whole + CO[1, k]
     misfit[...] = whole
+
+    fix(ITERS - 1, 1, first, 0)
 
     drain(ITERS - 1, 1)
 
@@ -705,21 +722,20 @@
             pltpu.VMEM((2, columns, 8, 128), F32),
             pltpu.VMEM((2, columns, 8, 128), F32),
             pltpu.VMEM((ITERS, NC, most, rows // NC, cols), F32),
-            dma((2, ITERS, NC)),
-            dma((2, ITERS, NC)),
-            dma((ITERS, NC, most)),
-            dma((ITERS, NC, most)),
-            dma((pairs, 3)),
-            dma((pairs, 3)),
-            dma((max(pairs - 1, 1), 3)),
-            dma((max(pairs - 1, 1), 3)),
-            dma((nshot - 1,)),
-            dma((nshot - 1,)),
+            dma((2, 2, NC)),
+            dma((2, 2, NC)),
+            dma((2, NC, most)),
+            dma((2, NC)),
+            dma((2,)),
+            dma((2,)),
+            dma((max(pairs - 1, 1), 2)),
+            dma((max(pairs - 1, 1), 2)),
+            dma((2,)),
             dma((2,)),
             dma((2,)),
             dma((2,)),
             dma((6,)),
-            dma((6,)),
+            dma((5,)),
         ],
         compiler_params=pltpu.CompilerParams(
             collective_id=0, has_side_effects=True, vmem_limit_bytes=52000000

time: 89 us -> 87.7 us (0.985)
  Pallas kernels: 88.2 us -> 86.7 us
    pallas_call x1, Pallas kernels: 85.5 us -> 84 us  [body(): pl.pallas_call(functools.partial(kernel, nshot, nspace), out_shape=(pltpu...]
where the time goes in v3:
time: 87.7 us; the launch traced here: 87.4 us
  Pallas kernels  86.7 us (99%)
    pallas_call x1, Pallas kernels, body(): pl.pallas_call(functools.partial(kernel, nshot, nspace), out_shape=(pltpu...  84 us
    pallas_call x1, Pallas kernels, body(): pl.pallas_call(functools.partial(finish, 0.5 / count), out_shape=(jax.Sha...  2.71 us

profile of v3, /device:TPU:0, one launch (start us, length us, event | category | flops | bytes accessed | tf_op | source)
XLA Modules:
  0.0 87.4 jit_solution(147219722136868812)
XLA Ops:
  0.6 84.0 %shard_map.120 = (f32[16,16,512]{2,1,0:T(8,128)S(1)}, f32[16,64,512]{2,1,0:T(8,128)S(1)}, f32[16,64,512]{2,1,0:T(8,128)S(1)}, f32[8,128]{1,0:T(8,128)S(1)}) custom-call(s32[1,256]{1,0:T(1,128)} %cells_h.1, s32[1,3]{1,0:T(1,128)} %source_h.1, f32[64]{0:T(128)} %table_h.1, f32[4,256]{1,0:T(4,128)} %bitcast.12, f32[16,64,512]{2,1,0:T(8,128)} %bitcast.9, ...), custom_call_target="tpu_custom_call" | custom-call | tf_op jit(solution)/shard_map/pallas_call | solution.py:682
  84.7 2.7 %shard_map.121 = (f32[16,16,512]{2,1,0:T(8,128)}, f32[16,64,512]{2,1,0:T(8,128)}, f32[16,64,512]{2,1,0:T(8,128)}, f32[1,1]{1,0:T(1,128)}) custom-call(f32[16,16,512]{2,1,0:T(8,128)S(1)} %get-tuple-element.12.grad, f32[16,64,512]{2,1,0:T(8,128)S(1)} %get-tuple-element.13.first, f32[16,64,512]{2,1,0:T(8,128)S(1)} %get-tuple-element.14.second, ...), custom_call_target="tpu_custom_call" | custom-call | tf_op jit(solution)/shard_map/pallas_call | solution.py:755

commit v4 on v3

--- a/solution.py
+++ b/solution.py
@@ -100,6 +100,7 @@
     s_recv,
     small_sem,
     local_sem,
+    ready,
 ):
     depth, rows, cols = cour.shape
     nrec = cells_row.shape[1]
@@ -111,7 +112,13 @@
     has_high = space < nspace - 1
 
     barrier = pltpu.get_barrier_semaphore()
-    near = ((-2, space >= 2), (-1, has_low), (1, has_high), (2, space < nspace - 2))
+    odd = lax.rem(space, 2)
+    has_under = space >= 2
+    has_over = space < nspace - 2
+    pl.semaphore_signal(
+        barrier, inc=1, device_id={"space": space + 1 - 2 * odd}, device_id_type=MESH
+    )
+    near = ((-2, has_under), (2, has_over))
     for d, there in near:
 
         @pl.when(there)
@@ -125,12 +132,15 @@
             barrier, inc=1, device_id={"shot": lax.rem(shot + d, nshot)}, device_id_type=MESH
         )
 
-    edge_low = pltpu.make_async_copy(
-        now_h.at[pl.ds(0, W)], E.at[1, pl.ds(W, W)], local_sem.at[4]
-    )
-    edge_high = pltpu.make_async_copy(
-        now_h.at[pl.ds(depth - W, W)], E.at[1, pl.ds(depth, W)], local_sem.at[4]
-    )
+    edges = [
+        pltpu.make_async_copy(
+            now_h.at[pl.ds(z, W), pl.ds(c * ych, ych)],
+            E.at[1, pl.ds(W + z, W), pl.ds(c * ych, ych)],
+            local_sem.at[4 + c],
+        )
+        for c in range(NC)
+        for z in (0, depth - W)
+    ]
     inner = depth - 2 * W
     in_now = pltpu.make_async_copy(
         now_h.at[pl.ds(W, inner)], E.at[1, pl.ds(2 * W, inner)], local_sem.at[0]
@@ -138,8 +148,8 @@
     in_later = pltpu.make_async_copy(later_h, E.at[0, pl.ds(W, depth)], local_sem.at[1])
     in_cour = pltpu.make_async_copy(cour_h, cour, local_sem.at[2])
     in_words = pltpu.make_async_copy(words_h, words, local_sem.at[3])
-    edge_low.start()
-    edge_high.start()
+    for copy in edges:
+        copy.start()
     in_words.start()
     in_now.start()
     in_cour.start()
@@ -160,13 +170,18 @@
     for copy in small:
         copy.start()
 
-    pltpu.make_async_copy(
-        now_h.at[pl.ds(0, 2 * W)], E.at[1, pl.ds(W, 2 * W)], local_sem.at[4]
-    ).wait()
     present = sum(there.astype(jnp.int32) for _, there in near)
-    pl.semaphore_wait(barrier, nshot - 1 + present)
-
-    odd = lax.rem(space, 2)
+    pl.semaphore_wait(barrier, nshot + present)
+    vouch = jnp.where(odd == 1, has_under, has_over)
+    await_vouch = jnp.where(odd == 1, has_over, has_under)
+
+    @pl.when(vouch)
+    def _():
+        pl.semaphore_signal(
+            ready, inc=1, device_id={"space": space + 2 - 4 * odd}, device_id_type=MESH
+        )
+
+
     column = space // 2
     columns = nspace // 2
     lean = W * (columns - 1 - column) // columns
@@ -218,7 +233,7 @@
             device_id_type=MESH,
         )
 
-    def send(t, c):
+    def send_beside(t, c):
         out = eased(n_out, 1, t, c)
         for p in range(most):
 
@@ -226,15 +241,30 @@
             def _():
                 detour(t, c, p).start()
 
+        @pl.when(odd == 0)
+        def _():
+            halo(t, c, 0, True, W).start()
+
+        @pl.when(odd == 1)
+        def _():
+            halo(t, c, 0, False, W).start()
+
+    def send_across(t, c):
+        out = eased(n_out, 1, t, c)
         for p in range(W):
-
-            @pl.when(jnp.logical_and(has_high, p >= odd * out))
+            here = p >= out
+
+            @pl.when(jnp.logical_and(here, jnp.logical_and(has_high, odd == 1)))
             def _():
                 halo(t, c, p, True).start()
 
-            @pl.when(jnp.logical_and(has_low, p >= (1 - odd) * out))
+            @pl.when(jnp.logical_and(here, jnp.logical_and(has_low, odd == 0)))
             def _():
                 halo(t, c, p, False).start()
+
+    def send(t, c):
+        send_beside(t, c)
+        send_across(t, c)
 
     def relay(t, c):
         n = eased(n_in, 0, t, c)
@@ -262,7 +292,19 @@
                 onward(t, c, 0, count).wait_send()
 
     for c in range(NC):
-        send(0, c)
+        pltpu.make_async_copy(
+            now_h.at[pl.ds(0, 2 * W), rows_of(c)],
+            E.at[1, pl.ds(W, 2 * W), rows_of(c)],
+            local_sem.at[4 + c],
+        ).wait()
+        send_beside(0, c)
+
+    @pl.when(await_vouch)
+    def _():
+        pl.semaphore_wait(ready, 1)
+
+    for c in range(NC):
+        send_across(0, c)
 
     @pl.loop(0, cols // 64)
     def _(i):
@@ -735,7 +777,8 @@
             dma((2,)),
             dma((2,)),
             dma((6,)),
-            dma((5,)),
+            dma((4 + NC,)),
+            pltpu.SemaphoreType.REGULAR,
         ],
         compiler_params=pltpu.CompilerParams(
             collective_id=0, has_side_effects=True, vmem_limit_bytes=52000000

time: 87.7 us -> 87.8 us (level)
  no operation moved by 1% of the time
where the time goes in v4:
time: 87.8 us; the launch traced here: 87.7 us
  Pallas kernels  86.9 us (99%)
    pallas_call x1, Pallas kernels, body(): pl.pallas_call(functools.partial(kernel, nshot, nspace), out_shape=(pltpu...  84.2 us
    pallas_call x1, Pallas kernels, body(): pl.pallas_call(functools.partial(finish, 0.5 / count), out_shape=(jax.Sha...  2.71 us

profile of v4, /device:TPU:0, one launch (start us, length us, event | category | flops | bytes accessed | tf_op | source)
XLA Modules:
  0.0 87.7 jit_solution(6374119547199465945)
XLA Ops:
  0.6 84.2 %shard_map.120 = (f32[16,16,512]{2,1,0:T(8,128)S(1)}, f32[16,64,512]{2,1,0:T(8,128)S(1)}, f32[16,64,512]{2,1,0:T(8,128)S(1)}, f32[8,128]{1,0:T(8,128)S(1)}) custom-call(s32[1,256]{1,0:T(1,128)} %cells_h.1, s32[1,3]{1,0:T(1,128)} %source_h.1, f32[64]{0:T(128)} %table_h.1, f32[4,256]{1,0:T(4,128)} %bitcast.12, f32[16,64,512]{2,1,0:T(8,128)} %bitcast.9, ...), custom_call_target="tpu_custom_call" | custom-call | tf_op jit(solution)/shard_map/pallas_call | solution.py:724
  84.8 2.7 %shard_map.121 = (f32[16,16,512]{2,1,0:T(8,128)}, f32[16,64,512]{2,1,0:T(8,128)}, f32[16,64,512]{2,1,0:T(8,128)}, f32[1,1]{1,0:T(1,128)}) custom-call(f32[16,16,512]{2,1,0:T(8,128)S(1)} %get-tuple-element.12.grad, f32[16,64,512]{2,1,0:T(8,128)S(1)} %get-tuple-element.13.first, f32[16,64,512]{2,1,0:T(8,128)S(1)} %get-tuple-element.14.second, ...), custom_call_target="tpu_custom_call" | custom-call | tf_op jit(solution)/shard_map/pallas_call | solution.py:798
